TPU v7x, 32 devices: a whole 2x2x4 slice. The times are simulated.
32 devices in a mesh: row: 4 (over z), col: 8 (over y, x, core).
Axes of the slice: x: 2, y: 2, z: 4, core: 2. Of those that a mesh axis runs over, the one named last changes fastest.
Arguments:
- fine_residual: bfloat16 [16, 524288], P(None, ('row', 'col')), may hold values from -6 to 6
- tiles_one: bfloat16 [8192, 128, 128], P(('row', 'col')), may hold values from -0.1875 to 0.1875
- pointers_one: int32 [4128], P(('row', 'col')), may hold values from 0 to 256, as said below
- columns_one: int32 [8192], P(('row', 'col')), may hold values from 0 to 1023, as said below
- points_one: int32 [131072], P(('col', 'row')), may hold values from 0 to 16383, as said below
- tiles_two: bfloat16 [4096, 128, 128], P(('row', 'col')), may hold values from -0.125 to 0.125
- pointers_two: int32 [2080], P(('row', 'col')), may hold values from 0 to 128, as said below
- columns_two: int32 [4096], P(('row', 'col')), may hold values from 0 to 127
- points_two: int32 [32768], P(('row', 'col')), may hold values from 0 to 4095, as said below
- tiles_three: bfloat16 [512, 128, 128], P(('row', 'col')), may hold values from -0.1875 to 0.1875
- pointers_three: int32 [288], P(('row', 'col')), may hold values from 0 to 16, as said below
- columns_three: int32 [512], P(('row', 'col')), may hold values from 0 to 63
- points_three: int32 [8192], P(('col', 'row')), may hold values from 0 to 1023, as said below
Outputs:
- coarse_one: bfloat16 [16, 131072], P(None, ('col', 'row'))
- coarse_two: bfloat16 [16, 32768], P(None, ('row', 'col'))
- coarse_three: bfloat16 [16, 8192], P(None, ('col', 'row'))
Inputs may be any that keep to these rules, and one draw needn't show every extreme that they name: `pointers_one`: each tile set's 128 + 1 pointers start at 0 and never fall; the last is that set's live slot count, at most 256; some set has 256 live slots. `pointers_two`: each tile set's 64 + 1 pointers start at 0 and never fall; the last is that set's live slot count, at most 128; some set has 128 live slots. `pointers_three`: each tile set's 8 + 1 pointers start at 0 and never fall; the last is that set's live slot count, at most 16; some set has 16 live slots. `columns_one`: among the live slots of one tile set, at most 32 name block columns with the same quotient by 128; some set reaches 32. `points_one`: values are distinct within each aligned run of 4096 entries. `points_two`: values are distinct within each aligned run of 1024 entries. `points_three`: values are distinct within each aligned run of 256 entries.
All inputs are finite; a program needn't handle non-finite values.
Results may differ from a plain program's by a relative error of at most 0.0057.
Values may be sent and summed in bfloat16 or wider, within the bound.
No kernel may reach another device: no remote copies, remote signals or barrier semaphores. Data moves between devices by JAX's collectives and lax.ppermute only.
A program may use at most 128 MiB of HBM per device.

v0:
```python
import jax
import jax.numpy as jnp
from jax import lax
from jax.sharding import PartitionSpec as P


def slot_layout(pointers, slot_count):
    block_count = pointers.shape[0] - 1
    positions = jnp.arange(slot_count, dtype=jnp.int32)
    is_live = positions < pointers[block_count]
    finished = jnp.sum((pointers[1:][None, :] <= positions[:, None]).astype(jnp.int32), axis=1)
    segment = jnp.where(is_live, finished, block_count)
    return (is_live, segment)


def block_sums(products, segment, block_count):
    summed = jax.ops.segment_sum(
        products, segment, num_segments=block_count + 1, indices_are_sorted=True
    )
    summed = summed[:block_count]
    return jnp.transpose(summed, (1, 0, 2)).reshape(summed.shape[1], block_count * summed.shape[2])


def group_products(tiles, fine_group, columns, segment, block_count):
    vector_count = fine_group.shape[0]
    tile_edge = tiles.shape[1]
    blocks = fine_group.reshape(vector_count, fine_group.shape[1] // tile_edge, tile_edge)
    picked = jnp.take(blocks, columns, axis=1)
    products = jnp.einsum("sij,vsj->svi", tiles, picked, preferred_element_type=jnp.float32)
    return block_sums(products, segment, block_count)


def add_points(partial_value, own_piece, points, position):
    injected = jnp.take(own_piece, points, axis=1).astype(jnp.float32)
    offset = position * points.shape[0]
    current = lax.dynamic_slice_in_dim(partial_value, offset, points.shape[0], 1)
    return lax.dynamic_update_slice_in_dim(partial_value, current + injected, offset, 1)


def on_device(
    fine_residual,
    tiles_one,
    pointers_one,
    columns_one,
    points_one,
    tiles_two,
    pointers_two,
    columns_two,
    points_two,
    tiles_three,
    pointers_three,
    columns_three,
    points_three,
):
    tile_edge = tiles_one.shape[1]
    vector_count = fine_residual.shape[0]
    slots_first = tiles_one.shape[0]
    blocks_first = pointers_one.shape[0] - 1
    live_first, segment_first = slot_layout(pointers_one, slots_first)
    peer_count = lax.axis_size("col")
    per_peer = slots_first // peer_count
    blocks_peer = fine_residual.shape[1] // tile_edge
    owner_peer = columns_one // blocks_peer
    within = columns_one % blocks_peer
    peer_ids = jnp.arange(peer_count, dtype=jnp.int32)
    peer_hits = ((owner_peer[:, None] == peer_ids[None, :]) & live_first[:, None]).astype(jnp.int32)
    peer_rank = jnp.sum(jnp.cumsum(peer_hits, axis=0) * peer_hits, axis=1) - 1
    target = jnp.where(live_first, owner_peer * per_peer + peer_rank, peer_count * per_peer)
    requests = jnp.zeros((peer_count * per_peer,), jnp.int32).at[target].set(within, mode="drop")
    requests = requests.reshape(peer_count, per_peer)
    own_blocks = jnp.transpose(
        fine_residual.reshape(vector_count, blocks_peer, tile_edge), (1, 0, 2)
    )
    found_blocks = jnp.take(
        own_blocks, lax.all_to_all(requests, "col", split_axis=0, concat_axis=0, tiled=True), axis=0
    )
    replies = lax.all_to_all(found_blocks, "col", split_axis=0, concat_axis=0, tiled=True)
    flat_replies = replies.reshape(peer_count * per_peer, vector_count, tile_edge)
    picked = jnp.take(flat_replies, jnp.minimum(target, peer_count * per_peer - 1), axis=0)
    products = jnp.einsum("sij,svj->svi", tiles_one, picked, preferred_element_type=jnp.float32)
    partial_one = block_sums(products, segment_first, blocks_first)
    partial_one = add_points(partial_one, fine_residual, points_one, lax.axis_index("row"))
    coarse_one = lax.psum_scatter(partial_one, "row", scatter_dimension=1, tiled=True).astype(
        jnp.bfloat16
    )
    group_one = lax.all_gather(coarse_one, "row", axis=1, tiled=True)
    segment_second = slot_layout(pointers_two, tiles_two.shape[0])[1]
    partial_two = group_products(
        tiles_two, group_one, columns_two, segment_second, pointers_two.shape[0] - 1
    )
    partial_two = add_points(partial_two, coarse_one, points_two, lax.axis_index("col"))
    coarse_two = lax.psum_scatter(partial_two, "col", scatter_dimension=1, tiled=True).astype(
        jnp.bfloat16
    )
    group_two = lax.all_gather(coarse_two, "col", axis=1, tiled=True)
    segment_third = slot_layout(pointers_three, tiles_three.shape[0])[1]
    partial_three = group_products(
        tiles_three, group_two, columns_three, segment_third, pointers_three.shape[0] - 1
    )
    partial_three = add_points(partial_three, coarse_two, points_three, lax.axis_index("row"))
    coarse_three = lax.psum_scatter(partial_three, "row", scatter_dimension=1, tiled=True).astype(
        jnp.bfloat16
    )
    return (coarse_one, coarse_two, coarse_three)


def solution(mesh):
    placed = (
        P(None, ("row", "col")),
        P(("row", "col"), None, None),
        P(("row", "col")),
        P(("row", "col")),
        P(("col", "row")),
        P(("row", "col"), None, None),
        P(("row", "col")),
        P(("row", "col")),
        P(("row", "col")),
        P(("row", "col"), None, None),
        P(("row", "col")),
        P(("row", "col")),
        P(("col", "row")),
    )
    return jax.shard_map(
        on_device,
        mesh=mesh,
        in_specs=placed,
        out_specs=(P(None, ("col", "row")), P(None, ("row", "col")), P(None, ("col", "row"))),
        check_vma=False,
    )
```

profile of v0, /device:TPU:0, one launch (start us, length us, event | category | flops | bytes accessed | tf_op | source)
XLA Modules:
  0.0 434.2 jit_solution(3455119433022537755)
XLA Ops:
  7.2 1.3 slice.33
  8.5 0.7 add_compare_fusion
  9.2 0.7 iota_compare_fusion.5
  9.8 0.7 and_select_fusion
  10.5 0.6 reduce-window.6
  11.4 0.7 compare_select_fusion.5
  12.1 1.4 scatter_custom_fusion
  13.5 0.7 all_to_all.13
  14.2 5.2 %all-to-all-start = ((s32[8,1,32]{2,1,0:T(1,128)}), s32[8,1,32]{2,1,0:T(1,128)S(1)}, u32[]{:S(2)}, u32[]{:S(2)}) async-start(s32[8,1,32]{2,1,0:T(1,128)} %all_to_all.13), calls=%async_computation | async-start | bytes 8192 | tf_op jit(solution)/shard_map/all_to_all | solution.py:75
  19.4 1.1 bitcast_bitcast_fusion
  20.5 3.5 all-to-all-done
  24.1 0.8 gather_fusion
  25.0 1.3 broadcast_select_fusion
  26.2 3.6 all-to-all-start.1
  29.9 3.1 copy.76
  33.0 16.9 %gather_fusion.2 = bf16[4096,16]{1,0:T(8,128)(2,1)} fusion(bf16[16,16384]{0,1:T(8,128)(2,1)} %copy.76, s32[4096]{0:T(1024)S(1)} %fusion.16), kind=kCustom, calls=%fused_computation.2 | custom fusion | bytes 278528 | tf_op jit(solution)/shard_map/jit(_take)/gather | solution.py:34
  50.0 0.7 compare_and_fusion.6
  50.8 0.7 compare_select_fusion.7
  51.4 0.8 gather_fusion.1
  52.3 9.3 %fusion.1 = f32[256,16,128]{2,1,0:T(8,128)} fusion(bf16[256,128,128]{2,1,0:T(8,128)(2,1)} %param.14, bf16[256,16,128]{2,1,0:T(8,128)(2,1)S(1)} %gather_fusion.1, pred[256]{0:T(512)(128)(4,1)S(1)} %get-tuple-element.21), kind=kOutput, calls=%fused_computation.14 | convolution fusion | flops 134742016 | bytes 11534592 | tf_op jit(solution)/shard_map/sij,svj->svi/dot_general | solution.py:80
  61.6 20.6 %scatter_fusion = f32[129,16,128]{2,1,0:T(8,128)S(1)} fusion(f32[129,16,128]{2,1,0:T(8,128)S(1)} %broadcast_in_dim.121, s32[256]{0:T(256)S(1)} %bitcast.75, f32[256,16,128]{2,1,0:T(8,128)} %fusion.1), kind=kCustom, calls=%fused_computation.8 | custom fusion | flops 524288 | bytes 6292480 | tf_op jit(solution)/shard_map/scatter-add | solution.py:17
  82.3 4.6 %copy.94 = f32[16,128,128]{0,2,1:T(8,128)} copy(f32[16,128,128]{2,0,1:T(8,128)S(1)} %slice_bitcast_fusion) | data formatting | bytes 2097152 | tf_op jit(solution)/shard_map/reshape | solution.py:21
  87.0 3.0 fusion
  90.7 0.6 slice.38
  91.4 0.7 fusion.22
  92.1 144.5 %reduce-scatter.4.cloned.1.call-done = f32[16,4096]{0,1:T(8,128)} async-done(((f32[16,16384]{0,1:T(8,128)}), f32[16,4096]{0,1:T(8,128)}) %reduce-scatter.4.cloned.1.call-update) | async-done | bytes 262160 | tf_op jit(solution)/shard_map/reduce_scatter | solution.py:83
  236.6 1.7 convert_element_type.35
  238.3 72.1 %all_gather.6 = bf16[16,16384]{0,1:T(8,128)(2,1)} all-gather(bf16[16,4096]{0,1:T(8,128)(2,1)S(1)} %convert_element_type.35), channel_id=1, replica_groups=mesh['row'=4,'col'=8] {'row'}, dimensions={1}, use_global_device_ids=true | all-gather | bytes 655360 | tf_op jit(solution)/shard_map/all_gather | solution.py:86
  310.4 3.5 copy.79
  313.9 0.7 gather_fusion.3
  314.6 4.5 %fusion.5 = f32[128,16,128]{2,1,0:T(8,128)S(1)} fusion(bf16[128,128,128]{2,1,0:T(8,128)(2,1)} %param.18, bf16[128,16,128]{2,1,0:T(8,128)(2,1)S(1)} %gather_fusion.3, pred[128]{0:T(512)(128)(4,1)S(1)} %compare_and_fusion.5), kind=kOutput, calls=%fused_computation.22 | convolution fusion | flops 67371008 | bytes 5767296 | tf_op jit(solution)/shard_map/sij,vsj->svi/dot_general | solution.py:29
  319.2 5.5 %scatter_fusion.1 = f32[65,16,128]{2,1,0:T(8,128)S(1)} fusion(f32[65,16,128]{2,1,0:T(8,128)S(1)} %broadcast_in_dim.133, s32[128]{0:T(128)S(1)} %fusion.22, f32[128,16,128]{2,1,0:T(8,128)S(1)} %fusion.5), kind=kCustom, calls=%fused_computation.9 | custom fusion | flops 262144 | bytes 3146240 | tf_op jit(solution)/shard_map/scatter-add | solution.py:17
  324.8 2.6 copy.96
  327.3 3.2 gather_fusion.4
  330.6 2.0 fusion.4
  332.8 0.6 slice.41
  333.4 0.6 fusion.23
  334.1 50.5 %reduce-scatter.6.cloned.1.call-done = f32[16,1024]{0,1:T(8,128)} async-done(((f32[16,8192]{0,1:T(8,128)}), f32[16,1024]{0,1:T(8,128)}) %reduce-scatter.6.cloned.1.call-update) | async-done | bytes 65552 | tf_op jit(solution)/shard_map/reduce_scatter | solution.py:92
  384.6 1.1 convert_element_type.38
  385.7 15.3 %all_gather.7 = bf16[16,8192]{0,1:T(8,128)(2,1)} all-gather(bf16[16,1024]{0,1:T(8,128)(2,1)S(1)} %convert_element_type.38), channel_id=1, replica_groups=mesh['row'=4,'col'=8] {'col'}, dimensions={1}, use_global_device_ids=true | all-gather | bytes 294912 | tf_op jit(solution)/shard_map/all_gather | solution.py:95
  401.0 1.9 copy.84
  403.9 1.2 scatter_fusion.2
  405.2 0.9 gather_fusion.6
  406.2 0.6 copy-done.3
  406.9 1.0 copy.88
  407.8 0.7 copy.89
  408.6 17.8 %reduce-scatter.8.cloned.1.call-done = f32[16,256]{1,0:T(8,128)} async-done(((f32[16,1024]{1,0:T(8,128)}), f32[16,256]{1,0:T(8,128)}) %reduce-scatter.8.cloned.1.call-update) | async-done | bytes 16400 | tf_op jit(solution)/shard_map/reduce_scatter | solution.py:101
  426.4 1.3 convert_element_type.41
  (72 shorter events, 3.4 us)
Async XLA Ops:
  7.2 396.3 %copy-start = (bf16[16,128,128]{2,1,0:T(8,128)(2,1)S(1)}, bf16[16,128,128]{2,1,0:T(8,128)(2,1)}, u32[]{:S(2)}) copy-start(bf16[16,128,128]{2,1,0:T(8,128)(2,1)} %param.22) | copy-start | bytes 1572868
  7.2 22.7 %copy-start.7 = (s32[129]{0:T(256)S(1)}, s32[129]{0:T(256)}, u32[]{:S(2)}) copy-start(s32[129]{0:T(256)} %param.15) | copy-start | bytes 1552
  7.2 22.8 %copy-start.1 = (bf16[16,16384]{1,0:T(8,128)(2,1)S(1)}, bf16[16,16384]{1,0:T(8,128)(2,1)}, u32[]{:S(2)}) copy-start(bf16[16,16384]{1,0:T(8,128)(2,1)} %param.13) | copy-start | bytes 1572868
  7.2 22.6 %copy-start.4 = (s32[4096]{0:T(1024)S(1)}, s32[4096]{0:T(1024)}, u32[]{:S(2)}) copy-start(s32[4096]{0:T(1024)} %param.17) | copy-start | bytes 49156
  14.2 9.8 %all-to-all-start = ((s32[8,1,32]{2,1,0:T(1,128)}), s32[8,1,32]{2,1,0:T(1,128)S(1)}, u32[]{:S(2)}, u32[]{:S(2)}) async-start(s32[8,1,32]{2,1,0:T(1,128)} %all_to_all.13), calls=%async_computation | async-start | bytes 8192 | tf_op jit(solution)/shard_map/all_to_all | solution.py:75
  26.2 25.2 %all-to-all-start.1 = ((bf16[8,32,16,128]{3,2,1,0:T(8,128)(2,1)}), bf16[8,32,16,128]{3,2,1,0:T(8,128)(2,1)S(1)}, u32[]{:S(2)}, u32[]{:S(2)}) async-start(bf16[8,32,16,128]{3,2,1,0:T(8,128)(2,1)} %broadcast_select_fusion), calls=%async_computation.1 | async-start | bytes 2097152 | tf_op jit(solution)/shard_map/all_to_all | solution.py:77
  29.8 206.8 %reduce-scatter.4.cloned.1.call-start = ((), (), s32[]{:S(2)}) async-start(), calls=%async_computation.5 | async-start | bytes 10485760 | tf_op jit(solution)/shard_map/reduce_scatter | solution.py:83
  82.3 4.6 %copy-start.2 = (bf16[4096,16]{1,0:T(8,128)(2,1)S(1)}, bf16[4096,16]{1,0:T(8,128)(2,1)}, u32[]{:S(2)}) copy-start(bf16[4096,16]{1,0:T(8,128)(2,1)} %gather_fusion.2) | copy-start | bytes 393220
  89.9 0.7 copy-start.8
  89.9 1.3 copy-start.9
  89.9 1.3 copy-start.11
  89.9 2.1 copy-start.6
  89.9 2.1 copy-start.5
  90.0 294.7 %reduce-scatter.6.cloned.1.call-start = ((), (), s32[]{:S(2)}) async-start(), calls=%async_computation.6 | async-start | bytes 4718592 | tf_op jit(solution)/shard_map/reduce_scatter | solution.py:92
  324.7 7.9 %copy-start.10 = (s32[9]{0:T(128)S(1)}, s32[9]{0:T(128)}, u32[]{:S(2)}) copy-start(s32[9]{0:T(128)} %param.23) | copy-start | bytes 112
  332.6 93.8 %reduce-scatter.8.cloned.1.call-start = ((), (), s32[]{:S(2)}) async-start(), calls=%async_computation.7 | async-start | bytes 81920 | tf_op jit(solution)/shard_map/reduce_scatter | solution.py:101
  406.2 0.6 copy-start.3
Sparse Core Ops, SparseCore 0:
  90.1 146.4 reduce-scatter.3
  332.7 51.8 reduce-scatter.5
  407.0 19.3 reduce-scatter.7
where the time goes:
time: 435 us; the launch traced here: 434 us
  waiting for transfers between devices  216 us (50%)
  blocking collectives  87.4 us (20%)
  local copies, waits for them, and re-layouts  49.2 us (11%)
  other arithmetic  44.1 us (10%)
  matrix products  14.2 us (3%)
  between operations  14.2 us (3%)
  starting transfers between devices  8.88 us (2%)
    reduce_scatter x1, waiting for transfers between devices, on_device(): lax.psum_scatter(partial_one, 'row', scatter_dimension=1, tiled=True)  144 us
    all_gather x1, blocking collectives, on_device(): group_one = lax.all_gather(coarse_one, 'row', axis=1, tiled=True)  72.1 us
    reduce_scatter x1, waiting for transfers between devices, on_device(): lax.psum_scatter(partial_two, 'col', scatter_dimension=1, tiled=True)  50.5 us
    scatter-add x3, other arithmetic, block_sums(): jax.ops.segment_sum(products, segment, num_segments=block_count + 1, indi...  27.3 us
    gather x3, local copies, waits for them, and re-layouts, add_points(): injected = jnp.take(own_piece, points, axis=1).astype(jnp.float32)  21 us
    reduce_scatter x1, waiting for transfers between devices, on_device(): lax.psum_scatter(partial_three, 'row', scatter_dimension=1, tiled=True)  17.8 us
    all_gather x1, blocking collectives, on_device(): group_two = lax.all_gather(coarse_two, 'col', axis=1, tiled=True)  15.3 us
    dot_general x1, matrix products, on_device(): jnp.einsum('sij,svj->svi', tiles_one, picked, preferred_element_type=jnp....  9.25 us
  transfers between devices with their start and end apart: 5, of which 4 were waited for; matrix products, arithmetic and copies ran while one was open for 6% of the time, Pallas kernels for 0%

commit v1 on v0

--- a/solution.py
+++ b/solution.py
@@ -83,7 +83,7 @@
     coarse_one = lax.psum_scatter(partial_one, "row", scatter_dimension=1, tiled=True).astype(
         jnp.bfloat16
     )
-    group_one = lax.all_gather(coarse_one, "row", axis=1, tiled=True)
+    group_one = jnp.concatenate(lax.all_gather(coarse_one, "row"), axis=1)
     segment_second = slot_layout(pointers_two, tiles_two.shape[0])[1]
     partial_two = group_products(
         tiles_two, group_one, columns_two, segment_second, pointers_two.shape[0] - 1

time: 435 us -> 375 us (0.86)
  blocking collectives: 87.4 us -> 30.2 us
    all_gather x1, blocking collectives: 72.1 us -> 16.1 us  [on_device(): group_one = jnp.concatenate(lax.all_gather(coarse_one, 'row'), axis=1)]
    reshape x2 -> x1, local copies, waits for them, and re-layouts: 5.37 us -> 0.79 us  [group_products(): fine_group.reshape(vector_count, fine_group.shape[1] // tile_edge, tile_e...]
  transfers between devices with their start and end apart: 5 -> 5, of which waited for: 4 -> 4; matrix products, arithmetic and copies ran while one was open for 6% -> 7% of each run, Pallas kernels for 0% -> 0%
where the time goes in v1:
time: 375 us; the launch traced here: 374 us
  waiting for transfers between devices  217 us (58%)
  local copies, waits for them, and re-layouts  45.2 us (12%)
  other arithmetic  44.1 us (12%)
  blocking collectives  30.2 us (8%)
  matrix products  14.2 us (4%)
  between operations  14.2 us (4%)
  starting transfers between devices  8.88 us (2%)
    reduce_scatter x1, waiting for transfers between devices, on_device(): lax.psum_scatter(partial_one, 'row', scatter_dimension=1, tiled=True)  144 us
    reduce_scatter x1, waiting for transfers between devices, on_device(): lax.psum_scatter(partial_two, 'col', scatter_dimension=1, tiled=True)  50 us
    scatter-add x3, other arithmetic, block_sums(): jax.ops.segment_sum(products, segment, num_segments=block_count + 1, indi...  27.3 us
    gather x3, local copies, waits for them, and re-layouts, add_points(): injected = jnp.take(own_piece, points, axis=1).astype(jnp.float32)  21 us
    reduce_scatter x1, waiting for transfers between devices, on_device(): lax.psum_scatter(partial_three, 'row', scatter_dimension=1, tiled=True)  18.9 us
    all_gather x1, blocking collectives, on_device(): group_one = jnp.concatenate(lax.all_gather(coarse_one, 'row'), axis=1)  16.1 us
    all_gather x1, blocking collectives, on_device(): group_two = lax.all_gather(coarse_two, 'col', axis=1, tiled=True)  14.1 us
    dot_general x1, matrix products, on_device(): jnp.einsum('sij,svj->svi', tiles_one, picked, preferred_element_type=jnp....  9.25 us
  transfers between devices with their start and end apart: 5, of which 4 were waited for; matrix products, arithmetic and copies ran while one was open for 7% of the time, Pallas kernels for 0%

profile of v1, /device:TPU:0, one launch (start us, length us, event | category | flops | bytes accessed | tf_op | source)
XLA Modules:
  0.0 373.7 jit_solution(717970555386842993)
XLA Ops:
  7.2 1.3 slice.33
  8.5 0.7 add_compare_fusion
  9.2 0.7 iota_compare_fusion.5
  9.8 0.7 and_select_fusion
  10.5 0.6 reduce-window.6
  11.4 0.7 compare_select_fusion.5
  12.1 1.4 scatter_custom_fusion
  13.5 0.7 all_to_all.13
  14.2 5.2 %all-to-all-start = ((s32[8,1,32]{2,1,0:T(1,128)}), s32[8,1,32]{2,1,0:T(1,128)S(1)}, u32[]{:S(2)}, u32[]{:S(2)}) async-start(s32[8,1,32]{2,1,0:T(1,128)} %all_to_all.13), calls=%async_computation | async-start | bytes 8192 | tf_op jit(solution)/shard_map/all_to_all | solution.py:75
  19.4 1.1 bitcast_bitcast_fusion
  20.5 3.5 all-to-all-done
  24.1 0.8 gather_fusion
  25.0 1.3 broadcast_select_fusion
  26.2 3.6 all-to-all-start.1
  29.9 3.1 copy.83
  33.0 16.9 %gather_fusion.2 = bf16[4096,16]{1,0:T(8,128)(2,1)} fusion(bf16[16,16384]{0,1:T(8,128)(2,1)} %copy.83, s32[4096]{0:T(1024)S(1)} %fusion.16), kind=kCustom, calls=%fused_computation.2 | custom fusion | bytes 278528 | tf_op jit(solution)/shard_map/jit(_take)/gather | solution.py:34
  50.0 0.7 compare_and_fusion.6
  50.8 0.7 compare_select_fusion.7
  51.4 0.8 gather_fusion.1
  52.3 9.3 %fusion.1 = f32[256,16,128]{2,1,0:T(8,128)} fusion(bf16[256,128,128]{2,1,0:T(8,128)(2,1)} %param.14, bf16[256,16,128]{2,1,0:T(8,128)(2,1)S(1)} %gather_fusion.1, pred[256]{0:T(512)(128)(4,1)S(1)} %get-tuple-element.21), kind=kOutput, calls=%fused_computation.14 | convolution fusion | flops 134742016 | bytes 11534592 | tf_op jit(solution)/shard_map/sij,svj->svi/dot_general | solution.py:80
  61.6 20.6 %scatter_fusion = f32[129,16,128]{2,1,0:T(8,128)S(1)} fusion(f32[129,16,128]{2,1,0:T(8,128)S(1)} %broadcast_in_dim.121, s32[256]{0:T(256)S(1)} %bitcast.77, f32[256,16,128]{2,1,0:T(8,128)} %fusion.1), kind=kCustom, calls=%fused_computation.8 | custom fusion | flops 524288 | bytes 6292480 | tf_op jit(solution)/shard_map/scatter-add | solution.py:17
  82.3 4.6 %copy.100 = f32[16,128,128]{0,2,1:T(8,128)} copy(f32[16,128,128]{2,0,1:T(8,128)S(1)} %slice_bitcast_fusion) | data formatting | bytes 2097152 | tf_op jit(solution)/shard_map/reshape | solution.py:21
  87.0 3.0 fusion
  90.0 0.6 copy-done.9
  90.7 0.6 slice.38
  91.4 0.7 fusion.22
  92.1 144.5 %reduce-scatter.4.cloned.1.call-done = f32[16,4096]{0,1:T(8,128)} async-done(((f32[16,16384]{0,1:T(8,128)}), f32[16,4096]{0,1:T(8,128)}) %reduce-scatter.4.cloned.1.call-update) | async-done | bytes 262160 | tf_op jit(solution)/shard_map/reduce_scatter | solution.py:83
  236.6 1.7 convert_element_type.35
  238.6 16.1 %all-gather = bf16[64,4096]{1,0:T(8,128)(2,1)S(1)} all-gather(bf16[16,4096]{1,0:T(8,128)(2,1)S(1)} %copy.96), channel_id=2, replica_groups=mesh['row'=4,'col'=8] {'row'}, dimensions={0}, use_global_device_ids=true | all-gather | bytes 655360 | tf_op jit(solution)/shard_map/all_gather | solution.py:86
  256.0 0.7 gather_fusion.3
  256.7 4.5 %fusion.5 = f32[128,16,128]{2,1,0:T(8,128)S(1)} fusion(bf16[128,128,128]{2,1,0:T(8,128)(2,1)} %param.18, bf16[128,16,128]{2,1,0:T(8,128)(2,1)S(1)} %gather_fusion.3, pred[128]{0:T(512)(128)(4,1)S(1)} %compare_and_fusion.5), kind=kOutput, calls=%fused_computation.22 | convolution fusion | flops 67371008 | bytes 5767296 | tf_op jit(solution)/shard_map/sij,vsj->svi/dot_general | solution.py:29
  261.3 5.5 %scatter_fusion.1 = f32[65,16,128]{2,1,0:T(8,128)S(1)} fusion(f32[65,16,128]{2,1,0:T(8,128)S(1)} %broadcast_in_dim.133, s32[128]{0:T(128)S(1)} %fusion.22, f32[128,16,128]{2,1,0:T(8,128)S(1)} %fusion.5), kind=kCustom, calls=%fused_computation.9 | custom fusion | flops 262144 | bytes 3146240 | tf_op jit(solution)/shard_map/scatter-add | solution.py:17
  266.9 2.6 copy.102
  269.4 3.2 gather_fusion.4
  272.7 2.0 fusion.4
  274.9 0.6 slice.41
  275.5 0.6 fusion.23
  276.2 50.0 %reduce-scatter.6.cloned.1.call-done = f32[16,1024]{0,1:T(8,128)} async-done(((f32[16,8192]{0,1:T(8,128)}), f32[16,1024]{0,1:T(8,128)}) %reduce-scatter.6.cloned.1.call-update) | async-done | bytes 65552 | tf_op jit(solution)/shard_map/reduce_scatter | solution.py:92
  326.2 1.1 convert_element_type.38
  327.3 14.1 %all_gather.11 = bf16[16,8192]{0,1:T(8,128)(2,1)S(1)} all-gather(bf16[16,1024]{0,1:T(8,128)(2,1)S(1)} %convert_element_type.38), channel_id=1, replica_groups=mesh['row'=4,'col'=8] {'col'}, dimensions={1}, use_global_device_ids=true | all-gather | bytes 294912 | tf_op jit(solution)/shard_map/all_gather | solution.py:95
  341.4 0.8 copy.92
  342.2 0.6 gather_fusion.5
  343.3 1.2 scatter_fusion.2
  344.6 0.9 gather_fusion.6
  345.6 0.6 copy-done.4
  346.2 0.7 copy.97
  347.0 18.9 %reduce-scatter.8.cloned.1.call-done = f32[16,256]{1,0:T(8,128)} async-done(((f32[16,1024]{1,0:T(8,128)}), f32[16,256]{1,0:T(8,128)}) %reduce-scatter.8.cloned.1.call-update) | async-done | bytes 16400 | tf_op jit(solution)/shard_map/reduce_scatter | solution.py:101
  365.8 1.3 convert_element_type.41
  (76 shorter events, 3.8 us)
Async XLA Ops:
  7.2 335.7 %copy-start = (bf16[16,128,128]{2,1,0:T(8,128)(2,1)S(1)}, bf16[16,128,128]{2,1,0:T(8,128)(2,1)}, u32[]{:S(2)}) copy-start(bf16[16,128,128]{2,1,0:T(8,128)(2,1)} %param.22) | copy-start | bytes 1572868
  7.2 22.7 %copy-start.8 = (s32[129]{0:T(256)S(1)}, s32[129]{0:T(256)}, u32[]{:S(2)}) copy-start(s32[129]{0:T(256)} %param.15) | copy-start | bytes 1552
  7.2 22.8 %copy-start.1 = (bf16[16,16384]{1,0:T(8,128)(2,1)S(1)}, bf16[16,16384]{1,0:T(8,128)(2,1)}, u32[]{:S(2)}) copy-start(bf16[16,16384]{1,0:T(8,128)(2,1)} %param.13) | copy-start | bytes 1572868
  7.2 22.6 %copy-start.5 = (s32[4096]{0:T(1024)S(1)}, s32[4096]{0:T(1024)}, u32[]{:S(2)}) copy-start(s32[4096]{0:T(1024)} %param.17) | copy-start | bytes 49156
  14.2 9.8 %all-to-all-start = ((s32[8,1,32]{2,1,0:T(1,128)}), s32[8,1,32]{2,1,0:T(1,128)S(1)}, u32[]{:S(2)}, u32[]{:S(2)}) async-start(s32[8,1,32]{2,1,0:T(1,128)} %all_to_all.13), calls=%async_computation | async-start | bytes 8192 | tf_op jit(solution)/shard_map/all_to_all | solution.py:75
  26.2 25.2 %all-to-all-start.1 = ((bf16[8,32,16,128]{3,2,1,0:T(8,128)(2,1)}), bf16[8,32,16,128]{3,2,1,0:T(8,128)(2,1)S(1)}, u32[]{:S(2)}, u32[]{:S(2)}) async-start(bf16[8,32,16,128]{3,2,1,0:T(8,128)(2,1)} %broadcast_select_fusion), calls=%async_computation.1 | async-start | bytes 2097152 | tf_op jit(solution)/shard_map/all_to_all | solution.py:77
  29.8 206.8 %reduce-scatter.4.cloned.1.call-start = ((), (), s32[]{:S(2)}) async-start(), calls=%async_computation.5 | async-start | bytes 10485760 | tf_op jit(solution)/shard_map/reduce_scatter | solution.py:83
  82.3 4.6 %copy-start.2 = (bf16[4096,16]{1,0:T(8,128)(2,1)S(1)}, bf16[4096,16]{1,0:T(8,128)(2,1)}, u32[]{:S(2)}) copy-start(bf16[4096,16]{1,0:T(8,128)(2,1)} %gather_fusion.2) | copy-start | bytes 393220
  89.9 0.7 copy-start.9
  89.9 1.3 copy-start.10
  89.9 1.3 copy-start.12
  89.9 2.1 copy-start.7
  89.9 2.1 copy-start.6
  90.0 236.3 %reduce-scatter.6.cloned.1.call-start = ((), (), s32[]{:S(2)}) async-start(), calls=%async_computation.6 | async-start | bytes 4718592 | tf_op jit(solution)/shard_map/reduce_scatter | solution.py:92
  238.6 22.6 %copy-start.3 = (bf16[16,4096]{1,0:T(8,128)(2,1)}, bf16[16,4096]{1,0:T(8,128)(2,1)S(1)}, u32[]{:S(2)}) copy-start(bf16[16,4096]{1,0:T(8,128)(2,1)S(1)} %copy.96) | copy-start | bytes 393220
  266.8 7.9 %copy-start.11 = (s32[9]{0:T(128)S(1)}, s32[9]{0:T(128)}, u32[]{:S(2)}) copy-start(s32[9]{0:T(128)} %param.23) | copy-start | bytes 112
  274.7 91.1 %reduce-scatter.8.cloned.1.call-start = ((), (), s32[]{:S(2)}) async-start(), calls=%async_computation.7 | async-start | bytes 81920 | tf_op jit(solution)/shard_map/reduce_scatter | solution.py:101
  345.6 0.6 copy-start.4
Sparse Core Ops, SparseCore 0:
  90.1 146.4 reduce-scatter.3
  274.8 51.3 reduce-scatter.5
  346.4 19.4 reduce-scatter.7
